TPU v7x, 32 devices: a whole 2x2x4 slice. The times are simulated.
32 devices in a mesh: league: 2 (over x), seq: 16 (over z, y, core).
Axes of the slice: x: 2, y: 2, z: 4, core: 2. Of those that a mesh axis runs over, the one named last changes fastest.
Arguments:
- queries: bfloat16 [6144, 1792], P(('league', 'seq')), parts along dimension 0, may hold values from -100 to 100
- key_rows: bfloat16 [6144, 256], P(('league', 'seq')), parts along dimension 0, may hold values from -4 to 4
- value_rows: bfloat16 [6144, 256], P(('league', 'seq')), parts along dimension 0, may hold values from -6 to 6
- residual: bfloat16 [6144, 3584], P(('league', 'seq')), parts along dimension 0, may hold values from -6 to 6
- out_weight: bfloat16 [1792, 3584], P('seq'), may hold values from -0.125 to 0.125
- norm_gain: float32 [3584], replicated, may hold values from 0.1 to 1.9
- value_head: float32 [3584], replicated, may hold values from -0.09375 to 0.09375
- valid_length: int32 [2], P('league'), parts along dimension 0, may hold values from 1537 to 3072
Outputs:
- stream: bfloat16 [6144, 3584], P(('league', 'seq')), parts along dimension 0
- values: float32 [6144], P(('league', 'seq')), parts along dimension 0
There are 2 independent parts, one for each index of `league`. A program takes and returns all parts, laid end to end along the dimension named above; an argument that names none is the same for every part. Nothing has to cross between parts.
All inputs are finite; a program needn't handle non-finite values.
Results may differ from a plain program's by a relative error of at most 0.0085.
Values may be sent and summed in bfloat16 or wider, within the bound.
A program may use at most 128 MiB of HBM per device.

v0:
```python
import math
import jax
import jax.numpy as jnp
from jax import lax
from jax.sharding import PartitionSpec as P

HEAD_DIM = 128
NEG_BIG = -1e30


def row_positions(row_index, tok_count):
    owner_dev = row_index // tok_count
    within = row_index % tok_count
    return owner_dev * tok_count + within


def attend_block(
    carried, key_block, value_block, key_pos, query_grid, query_pos, query_limit, score_scale
):

    def run_block(carry_in):
        running_max, running_sum, running_out = carry_in
        scores = (
            jnp.einsum("qgrd,kgd->qgrk", query_grid, key_block, preferred_element_type=jnp.float32)
            * score_scale
        )
        allowed = key_pos[None, None, None, :] <= query_pos[:, None, None, None]
        new_max = jnp.maximum(running_max, jnp.max(jnp.where(allowed, scores, NEG_BIG), axis=-1))
        shrink = jnp.exp(running_max - new_max)
        weights = jnp.where(allowed, jnp.exp(scores - new_max[..., None]), 0.0)
        running_sum = running_sum * shrink + jnp.sum(weights, axis=-1)
        running_out = running_out * shrink[..., None] + jnp.einsum(
            "qgrk,kgd->qgrd",
            weights.astype(jnp.bfloat16),
            value_block,
            preferred_element_type=jnp.float32,
        )
        return (new_max, running_sum, running_out)

    def keep_block(carry_in):
        return carry_in

    needed = jnp.min(key_pos) <= query_limit
    return lax.cond(needed, run_block, keep_block, carried)


def attend_piece(
    carried, key_piece, value_piece, key_pos, query_grid, query_pos, query_limit, score_scale
):
    piece_rows = key_piece.shape[0]
    block_rows = math.gcd(piece_rows, 512)
    block_count = piece_rows // block_rows
    groups = key_piece.shape[1] // HEAD_DIM
    key_blocks = key_piece.reshape(block_count, block_rows, groups, HEAD_DIM)
    value_blocks = value_piece.reshape(block_count, block_rows, groups, HEAD_DIM)
    pos_blocks = key_pos.reshape(block_count, block_rows)

    def one_block(carry_in, inputs):
        return (
            attend_block(
                carry_in,
                inputs[0],
                inputs[1],
                inputs[2],
                query_grid,
                query_pos,
                query_limit,
                score_scale,
            ),
            None,
        )

    carried, unused = lax.scan(one_block, carried, (key_blocks, value_blocks, pos_blocks))
    return carried


def per_device(
    queries, key_rows, value_rows, residual, out_weight, norm_gain, value_head, valid_length
):
    device = lax.axis_index("seq")
    tok_count = queries.shape[0]
    valid_upto = valid_length[0]
    groups = key_rows.shape[1] // HEAD_DIM
    repeats = queries.shape[1] // key_rows.shape[1]
    score_scale = HEAD_DIM ** (-0.5)
    local_rows = jnp.arange(tok_count, dtype=jnp.int32)
    query_pos = row_positions(device * tok_count + local_rows, tok_count)
    query_ok = query_pos < valid_upto
    query_limit = jnp.max(jnp.where(query_ok, query_pos, -1))
    query_grid = queries.reshape(tok_count, groups, repeats, HEAD_DIM)
    start_state = (
        jnp.full((tok_count, groups, repeats), NEG_BIG, jnp.float32),
        jnp.zeros((tok_count, groups, repeats), jnp.float32),
        jnp.zeros((tok_count, groups, repeats, HEAD_DIM), jnp.float32),
    )
    key_piece = lax.all_gather(key_rows, "seq", axis=0, tiled=True)
    key_pos = row_positions(jnp.arange(key_piece.shape[0], dtype=jnp.int32), tok_count)
    carried = attend_piece(
        start_state,
        key_piece,
        lax.all_gather(value_rows, "seq", axis=0, tiled=True),
        key_pos,
        query_grid,
        query_pos,
        query_limit,
        score_scale,
    )
    running_max, running_sum, running_out = carried
    safe_sum = jnp.where(query_ok[:, None, None], running_sum, 1.0)
    attended = jnp.where(query_ok[:, None, None, None], running_out / safe_sum[..., None], 0.0)
    attended = attended.reshape(tok_count, groups * repeats * HEAD_DIM).astype(jnp.bfloat16)
    whole_weight = lax.all_gather(out_weight, "seq", axis=0, tiled=True)
    projected = jnp.dot(attended, whole_weight, preferred_element_type=jnp.float32)
    stream = (residual.astype(jnp.float32) + projected).astype(jnp.bfloat16)
    widened = stream.astype(jnp.float32)
    normed = widened * lax.rsqrt(jnp.mean(widened * widened, axis=-1, keepdims=True) + 1e-06)
    scored = jnp.sum(normed * (norm_gain * value_head)[None, :], axis=-1)
    natural_pos = device * tok_count + local_rows
    scored = jnp.where(natural_pos < valid_upto, scored, 0.0)
    return (stream, scored)


def solution(mesh):
    placed = (
        P(("league", "seq"), None),
        P(("league", "seq"), None),
        P(("league", "seq"), None),
        P(("league", "seq"), None),
        P("seq", None),
        P(),
        P(),
        P("league"),
    )
    return jax.shard_map(
        per_device,
        mesh=mesh,
        in_specs=placed,
        out_specs=(P(("league", "seq"), None), P(("league", "seq"))),
        check_vma=False,
    )
```

profile of v0, /device:TPU:0, one launch (start us, length us, event | category | flops | bytes accessed | tf_op | source)
XLA Modules:
  0.0 211.8 jit_solution(4323758560684722332)
XLA Ops:
  7.2 0.7 all-gather.4.cloned.1.call-update
  8.0 0.7 all-gather.6.cloned.1.call-update
  8.7 0.7 all-gather.8.cloned.1.call-update
  10.1 1.9 reshape.101
  12.9 39.7 %all-gather.4.cloned.1.call-done = bf16[3072,256]{1,0:T(8,128)(2,1)} async-done(((bf16[192,256]{1,0:T(8,128)(2,1)}), bf16[3072,256]{1,0:T(8,128)(2,1)}) %all-gather.4.cloned.1.call-update) | async-done | bytes 1572880 | tf_op jit(solution)/shard_map/all_gather | solution.py:96
  52.6 2.4 %reshape.100 = bf16[6,512,2,128]{3,2,1,0:T(2,128)(2,1)S(1)} reshape(bf16[3072,256]{1,0:T(8,128)(2,1)} %all-gather.4.cloned.1.call-done) | data formatting | bytes 3145728 | tf_op jit(solution)/shard_map/reshape | solution.py:54
  55.0 1.4 copy.10
  56.4 36.8 %all-gather.6.cloned.1.call-done = bf16[3072,256]{1,0:T(8,128)(2,1)} async-done(((bf16[192,256]{1,0:T(8,128)(2,1)}), bf16[3072,256]{1,0:T(8,128)(2,1)}) %all-gather.6.cloned.1.call-update) | async-done | bytes 1572880 | tf_op jit(solution)/shard_map/all_gather | solution.py:101
  93.3 2.4 %reshape.102 = bf16[6,512,2,128]{3,2,1,0:T(2,128)(2,1)S(1)} reshape(bf16[3072,256]{1,0:T(8,128)(2,1)} %all-gather.6.cloned.1.call-done) | data formatting | bytes 3145728 | tf_op jit(solution)/shard_map/reshape | solution.py:55
  95.6 1.4 copy.12
  97.2 19.7 %while.15 = (s32[]{:T(128)}, f32[192,2,7]{0,2,1:T(8,128)S(1)}, f32[192,2,7]{0,2,1:T(8,128)S(1)}, f32[192,2,7,128]{3,0,2,1:T(8,128)S(1)}, s32[6,512]{1,0:T(8,128)...) while((s32[]{:T(128)}, f32[192,2,7]{0,2,1:T(8,128)S(1)}, ...), condition=%wide.region_7.8_spmd.clone, body=%wide.region_1.7_spmd.clone.sunk | while | flops 720577664 | bytes 21064692 | solution.py:73
  97.2 0.7 fusion.52
  99.3 6.9 %conditional.3 = ((f32[192,2,7]{0,2,1:T(8,128)S(1)}, f32[192,2,7]{0,2,1:T(8,128)S(1)}, f32[192,2,7,128]{3,0,2,1:T(8,128)S(1)})) conditional(s32[]{:T(128)} %convert_element_type.48, (f32[192,2,7]{0,2,1:T(8,128)S(1)}, f32[192,2,7]{0,2,1:T(8,128)S(1)}, f32[192,2,7,128]{3,0,2,1:T(8,128)S(1)}) %tuple.53, (s32[1,512]{1,0:T(1,128)S(1)}, ...), branch_computations={%region_3.3_spmd, %region_4.6_spmd.clone} | conditional | flops 720575808 | bytes 21056228 | solution.py:44
  99.5 2.0 fusion.2
  101.5 1.8 fusion.6
  103.3 2.9 %fusion.16 = f32[192,2,7,128]{3,0,2,1:T(8,128)S(1)} fusion(f32[2,512,192,7]{1,2,3,0:T(8,128)S(1)} %get-tuple-element.265, f32[192,2,7]{0,2,1:T(8,128)S(1)} %max.5, pred[192,512]{1,0:T(8,128)(4,1)S(1)} %broadcast_compare_fusion, f32[192,2,7,128]{3,0,2,1:T(8,128)S(1)} %get-tuple-element.208, f32[192,2,7]{0,2,1:T(8,128)S(1)} %get-tuple-element.261, ...), kind=kOutput, calls=%fused_computation.14 | convolution fusion | flops 358514688 | bytes 8640000 | tf_op jit(solution)/shard_map/while/body/eval_jaxpr/cond/branch_1_fun/qgrk,kgd->qgrd/dot_general | solution.py:32
  106.2 0.7 fusion.52
  108.3 0.7 fusion.52
  110.5 0.7 fusion.52
  112.6 0.7 fusion.52
  114.8 0.7 fusion.52
  117.9 0.7 convert_element_type.25
  118.6 77.7 %all-gather.8.cloned.1.call-done = bf16[1792,3584]{1,0:T(8,128)(2,1)} async-done(((bf16[112,3584]{1,0:T(8,128)(2,1)}), bf16[1792,3584]{1,0:T(8,128)(2,1)}) %all-gather.8.cloned.1.call-update) | async-done | bytes 12845072 | tf_op jit(solution)/shard_map/all_gather | solution.py:112
  196.3 7.8 %fusion.35 = (f32[192]{0:T(256)S(1)}, bf16[192,3584]{1,0:T(8,128)(2,1)S(1)}) fusion(bf16[192,1792]{1,0:T(8,128)(2,1)S(1)} %convert_element_type.25, bf16[1792,3584]{1,0:T(8,128)(2,1)} %all-gather.8.cloned.1.call-done, bf16[192,3584]{1,0:T(8,128)(2,1)} %param.15), kind=kOutput, calls=%fused_computation.42 | convolution fusion | flops 2470379264 | bytes 16286464 | tf_op jit(solution)/shard_map/dot_general | solution.py:113
  (63 shorter events, 3.6 us)
Async XLA Ops:
  7.2 5.0 %copy-start.1 = (f32[3584]{0:T(1024)S(1)}, f32[3584]{0:T(1024)}, u32[]{:S(2)}) copy-start(f32[3584]{0:T(1024)} %param.17) | copy-start | bytes 43012
  7.2 5.0 %copy-start.2 = (f32[3584]{0:T(1024)S(1)}, f32[3584]{0:T(1024)}, u32[]{:S(2)}) copy-start(f32[3584]{0:T(1024)} %param.18) | copy-start | bytes 43012
  7.2 45.4 %all-gather.4.cloned.1.call-start = ((), (), s32[]{:S(2)}) async-start(), calls=%async_computation | async-start | bytes 1671168 | tf_op jit(solution)/shard_map/all_gather | solution.py:96
  7.9 85.3 %all-gather.6.cloned.1.call-start = ((), (), s32[]{:S(2)}) async-start(), calls=%async_computation.1 | async-start | bytes 1671168 | tf_op jit(solution)/shard_map/all_gather | solution.py:101
  8.7 187.7 %all-gather.8.cloned.1.call-start = ((), (), s32[]{:S(2)}) async-start(), calls=%async_computation.2 | async-start | bytes 13647872 | tf_op jit(solution)/shard_map/all_gather | solution.py:112
  204.1 1.1 copy-start
Sparse Core Ops, SparseCore 0:
  10.3 42.3 all-gather.3
  54.9 38.2 all-gather.5
  95.5 100.7 all-gather.7
where the time goes:
time: 212 us
  waiting for transfers between devices  156 us (74%)
  between operations  14.6 us (7%)
  matrix products  12.7 us (6%)
  local copies, waits for them, and re-layouts  11 us (5%)
  other arithmetic  8.68 us (4%)
  loops' own time  8.39 us (4%)
    all_gather x1, waiting for transfers between devices, per_device(): whole_weight = lax.all_gather(out_weight, 'seq', axis=0, tiled=True)  77.7 us
    all_gather x1, waiting for transfers between devices, per_device(): key_piece = lax.all_gather(key_rows, 'seq', axis=0, tiled=True)  39.7 us
    all_gather x1, waiting for transfers between devices, per_device(): lax.all_gather(value_rows, 'seq', axis=0, tiled=True)  36.8 us
    another operation x1, loops' own time, attend_piece(): lax.scan(one_block, carried, (key_blocks, value_blocks, pos_blocks))  8.26 us
    dot_general x1, matrix products, per_device(): jnp.dot(attended, whole_weight, preferred_element_type=jnp.float32)  7.8 us
    reduce_min x6, other arithmetic, attend_block(): needed = jnp.min(key_pos) <= query_limit  4.3 us
  transfers between devices with their start and end apart: 3, of which 3 were waited for; matrix products, arithmetic and copies ran while one was open for 11% of the time, Pallas kernels for 0%

commit v1 on v0

--- a/solution.py
+++ b/solution.py
@@ -109,7 +109,12 @@
     safe_sum = jnp.where(query_ok[:, None, None], running_sum, 1.0)
     attended = jnp.where(query_ok[:, None, None, None], running_out / safe_sum[..., None], 0.0)
     attended = attended.reshape(tok_count, groups * repeats * HEAD_DIM).astype(jnp.bfloat16)
-    whole_weight = lax.all_gather(out_weight, "seq", axis=0, tiled=True)
+    ring = [out_weight]
+    for hop in range(15):
+        ring.append(lax.ppermute(ring[-1], "seq", [(dev, (dev + 1) % 16) for dev in range(16)]))
+    whole_weight = jnp.roll(
+        jnp.concatenate(ring[::-1], axis=0), (lax.axis_index("seq") + 1) * ring[0].shape[0], axis=0
+    )
     projected = jnp.dot(attended, whole_weight, preferred_element_type=jnp.float32)
     stream = (residual.astype(jnp.float32) + projected).astype(jnp.bfloat16)
     widened = stream.astype(jnp.float32)

time: 212 us -> 366 us (1.73)
  the two profiles are of different devices: /device:TPU:0 before, /device:TPU:31 now
where the time goes in v1:
time: 366 us; the launch traced here: 364 us
  waiting for transfers between devices  133 us (36%)
  local copies, waits for them, and re-layouts  82.6 us (23%)
  starting transfers between devices  68.5 us (19%)
  matrix products  37.5 us (10%)
  other arithmetic  19.6 us (5%)
  between operations  14.9 us (4%)
  loops' own time  8.57 us (2%)
    ppermute x15, waiting for transfers between devices, per_device(): lax.ppermute(ring[-1], 'seq', [(dev, (dev + 1) % 16) for dev in range(16)])  133 us
    unnamed x74, local copies, waits for them, and re-layouts  70.9 us
    ppermute x15, starting transfers between devices, per_device(): lax.ppermute(ring[-1], 'seq', [(dev, (dev + 1) % 16) for dev in range(16)])  68.4 us
    dot_general x6, matrix products, run_block(): jnp.einsum('qgrk,kgd->qgrd', weights.astype(jnp.bfloat16), value_block, p...  16.8 us
    dot_general x6, matrix products, run_block(): jnp.einsum('qgrd,kgd->qgrk', query_grid, key_block, preferred_element_typ...  12.2 us
    reduce_sum x6, other arithmetic, run_block(): running_sum = running_sum * shrink + jnp.sum(weights, axis=-1)  10.6 us
    dot_general x1, matrix products, per_device(): jnp.dot(attended, whole_weight, preferred_element_type=jnp.float32)  8.51 us
    another operation x1, loops' own time, attend_piece(): lax.scan(one_block, carried, (key_blocks, value_blocks, pos_blocks))  8.21 us
  transfers between devices with their start and end apart: 17, of which 13 were waited for; matrix products, arithmetic and copies ran while one was open for 17% of the time, Pallas kernels for 0%

profile of v1, /device:TPU:31, one launch (start us, length us, event | category | flops | bytes accessed | tf_op | source)
XLA Modules:
  0.0 364.5 jit_solution(12840812587522723388)
XLA Ops:
  7.7 9.4 %collective-permute-done = bf16[112,3584]{1,0:T(8,128)(2,1)S(1)} collective-permute-done((bf16[112,3584]{1,0:T(8,128)(2,1)}, bf16[112,3584]{1,0:T(8,128)(2,1)S(1)}, u32[]{:S(2)}, u32[]{:S(2)}) %collective-permute-start) | collective-permute-done | bytes 802848 | tf_op jit(solution)/shard_map/ppermute | solution.py:114
  23.1 9.1 %collective-permute-done.1 = bf16[112,3584]{1,0:T(8,128)(2,1)S(1)} collective-permute-done((bf16[112,3584]{1,0:T(8,128)(2,1)S(1)}, bf16[112,3584]{1,0:T(8,128)(2,1)S(1)}, u32[]{:S(2)}, u32[]{:S(2)}) %collective-permute-start.1) | collective-permute-done | bytes 802848 | tf_op jit(solution)/shard_map/ppermute | solution.py:114
  38.3 9.1 %collective-permute-done.2 = bf16[112,3584]{1,0:T(8,128)(2,1)S(1)} collective-permute-done((bf16[112,3584]{1,0:T(8,128)(2,1)S(1)}, bf16[112,3584]{1,0:T(8,128)(2,1)S(1)}, u32[]{:S(2)}, u32[]{:S(2)}) %collective-permute-start.2) | collective-permute-done | bytes 802848 | tf_op jit(solution)/shard_map/ppermute | solution.py:114
  53.5 9.1 %collective-permute-done.3 = bf16[112,3584]{1,0:T(8,128)(2,1)S(1)} collective-permute-done((bf16[112,3584]{1,0:T(8,128)(2,1)S(1)}, bf16[112,3584]{1,0:T(8,128)(2,1)S(1)}, u32[]{:S(2)}, u32[]{:S(2)}) %collective-permute-start.3) | collective-permute-done | bytes 802848 | tf_op jit(solution)/shard_map/ppermute | solution.py:114
  68.7 9.1 %collective-permute-done.4 = bf16[112,3584]{1,0:T(8,128)(2,1)S(1)} collective-permute-done((bf16[112,3584]{1,0:T(8,128)(2,1)S(1)}, bf16[112,3584]{1,0:T(8,128)(2,1)S(1)}, u32[]{:S(2)}, u32[]{:S(2)}) %collective-permute-start.4) | collective-permute-done | bytes 802848 | tf_op jit(solution)/shard_map/ppermute | solution.py:114
  83.9 9.1 %collective-permute-done.5 = bf16[112,3584]{1,0:T(8,128)(2,1)S(1)} collective-permute-done((bf16[112,3584]{1,0:T(8,128)(2,1)S(1)}, bf16[112,3584]{1,0:T(8,128)(2,1)S(1)}, u32[]{:S(2)}, u32[]{:S(2)}) %collective-permute-start.5) | collective-permute-done | bytes 802848 | tf_op jit(solution)/shard_map/ppermute | solution.py:114
  98.3 9.0 %collective-permute-done.6 = bf16[112,3584]{1,0:T(8,128)(2,1)S(1)} collective-permute-done((bf16[112,3584]{1,0:T(8,128)(2,1)S(1)}, bf16[112,3584]{1,0:T(8,128)(2,1)S(1)}, u32[]{:S(2)}, u32[]{:S(2)}) %collective-permute-start.6) | collective-permute-done | bytes 802848 | tf_op jit(solution)/shard_map/ppermute | solution.py:114
  107.3 5.3 %collective-permute-start.7 = (bf16[112,3584]{1,0:T(8,128)(2,1)S(1)}, bf16[112,3584]{1,0:T(8,128)(2,1)S(1)}, u32[]{:S(2)}, u32[]{:S(2)}) collective-permute-start(bf16[112,3584]{1,0:T(8,128)(2,1)S(1)} %collective-permute-done.6), channel_id=1, source_target_pairs={{0,1},{1,2},{2,3},{3,4},{4,5},{5,6},{6,7},{7,8},{8,9},{9,10},{10,1... | collective-permute-start | bytes 2408456 | tf_op jit(solution)/shard_map/ppermute | solution.py:114
  112.6 9.8 %collective-permute-done.7 = bf16[112,3584]{1,0:T(8,128)(2,1)S(1)} collective-permute-done((bf16[112,3584]{1,0:T(8,128)(2,1)S(1)}, bf16[112,3584]{1,0:T(8,128)(2,1)S(1)}, u32[]{:S(2)}, u32[]{:S(2)}) %collective-permute-start.7) | collective-permute-done | bytes 802848 | tf_op jit(solution)/shard_map/ppermute | solution.py:114
  128.5 15.4 %collective-permute-done.8 = bf16[112,3584]{1,0:T(8,128)(2,1)S(1)} collective-permute-done((bf16[112,3584]{1,0:T(8,128)(2,1)S(1)}, bf16[112,3584]{1,0:T(8,128)(2,1)S(1)}, u32[]{:S(2)}, u32[]{:S(2)}) %collective-permute-start.8) | collective-permute-done | bytes 802848 | tf_op jit(solution)/shard_map/ppermute | solution.py:114
  150.1 9.1 %collective-permute-done.9 = bf16[112,3584]{1,0:T(8,128)(2,1)S(1)} collective-permute-done((bf16[112,3584]{1,0:T(8,128)(2,1)S(1)}, bf16[112,3584]{1,0:T(8,128)(2,1)S(1)}, u32[]{:S(2)}, u32[]{:S(2)}) %collective-permute-start.9) | collective-permute-done | bytes 802848 | tf_op jit(solution)/shard_map/ppermute | solution.py:114
  164.4 9.1 %collective-permute-done.10 = bf16[112,3584]{1,0:T(8,128)(2,1)S(1)} collective-permute-done((bf16[112,3584]{1,0:T(8,128)(2,1)S(1)}, bf16[112,3584]{1,0:T(8,128)(2,1)S(1)}, u32[]{:S(2)}, u32[]{:S(2)}) %collective-permute-start.10) | collective-permute-done | bytes 802848 | tf_op jit(solution)/shard_map/ppermute | solution.py:114
  173.5 5.3 %collective-permute-start.11 = (bf16[112,3584]{1,0:T(8,128)(2,1)S(1)}, bf16[112,3584]{1,0:T(8,128)(2,1)S(1)}, u32[]{:S(2)}, u32[]{:S(2)}) collective-permute-start(bf16[112,3584]{1,0:T(8,128)(2,1)S(1)} %collective-permute-done.10), channel_id=1, source_target_pairs={{0,1},{1,2},{2,3},{3,4},{4,5},{5,6},{6,7},{7,8},{8,9},{9,10},{10,1... | collective-permute-start | bytes 2408456 | tf_op jit(solution)/shard_map/ppermute | solution.py:114
  178.8 9.8 %collective-permute-done.11 = bf16[112,3584]{1,0:T(8,128)(2,1)S(1)} collective-permute-done((bf16[112,3584]{1,0:T(8,128)(2,1)S(1)}, bf16[112,3584]{1,0:T(8,128)(2,1)S(1)}, u32[]{:S(2)}, u32[]{:S(2)}) %collective-permute-start.11) | collective-permute-done | bytes 802848 | tf_op jit(solution)/shard_map/ppermute | solution.py:114
  194.6 15.4 %collective-permute-done.12 = bf16[112,3584]{1,0:T(8,128)(2,1)} collective-permute-done((bf16[112,3584]{1,0:T(8,128)(2,1)S(1)}, bf16[112,3584]{1,0:T(8,128)(2,1)}, u32[]{:S(2)}, u32[]{:S(2)}) %collective-permute-start.12) | collective-permute-done | bytes 802848 | tf_op jit(solution)/shard_map/ppermute | solution.py:114
  210.1 5.3 %collective-permute-start.13 = (bf16[112,3584]{1,0:T(8,128)(2,1)}, bf16[112,3584]{1,0:T(8,128)(2,1)}, u32[]{:S(2)}, u32[]{:S(2)}) collective-permute-start(bf16[112,3584]{1,0:T(8,128)(2,1)} %collective-permute-done.12), channel_id=1, source_target_pairs={{0,1},{1,2},{2,3},{3,4},{4,5},{5,6},{6,7},{7,8},{8,9},{9,10},{10,1... | collective-permute-start | bytes 2408456 | tf_op jit(solution)/shard_map/ppermute | solution.py:114
  230.1 53.6 %while.15 = (s32[]{:T(128)}, f32[192,2,7]{0,2,1:T(8,128)S(1)}, f32[192,2,7]{0,2,1:T(8,128)S(1)}, f32[192,2,7,128]{3,0,2,1:T(8,128)S(1)}, s32[6,512]{1,0:T(8,128)...) while((s32[]{:T(128)}, f32[192,2,7]{0,2,1:T(8,128)S(1)}, ...), condition=%wide.region_7.8_spmd.clone, body=%wide.region_1.7_spmd.clone.sunk | while | flops 720577664 | bytes 21064692 | solution.py:73
  232.2 6.8 %conditional.3 = ((f32[192,2,7]{0,2,1:T(8,128)S(1)}, f32[192,2,7]{0,2,1:T(8,128)S(1)}, f32[192,2,7,128]{3,0,2,1:T(8,128)S(1)})) conditional(s32[]{:T(128)} %convert_element_type.48, (f32[192,2,7]{0,2,1:T(8,128)S(1)}, f32[192,2,7]{0,2,1:T(8,128)S(1)}, f32[192,2,7,128]{3,0,2,1:T(8,128)S(1)}) %tuple.53, (s32[1,512]{1,0:T(1,128)S(1)}, ...), branch_computations={%region_3.3_spmd, %region_4.6_spmd.clone} | conditional | flops 720575808 | bytes 21056228 | solution.py:44
  241.1 6.8 %conditional.3 = ((f32[192,2,7]{0,2,1:T(8,128)S(1)}, f32[192,2,7]{0,2,1:T(8,128)S(1)}, f32[192,2,7,128]{3,0,2,1:T(8,128)S(1)})) conditional(s32[]{:T(128)} %convert_element_type.48, (f32[192,2,7]{0,2,1:T(8,128)S(1)}, f32[192,2,7]{0,2,1:T(8,128)S(1)}, f32[192,2,7,128]{3,0,2,1:T(8,128)S(1)}) %tuple.53, (s32[1,512]{1,0:T(1,128)S(1)}, ...), branch_computations={%region_3.3_spmd, %region_4.6_spmd.clone} | conditional | flops 720575808 | bytes 21056228 | solution.py:44
  250.1 6.8 %conditional.3 = ((f32[192,2,7]{0,2,1:T(8,128)S(1)}, f32[192,2,7]{0,2,1:T(8,128)S(1)}, f32[192,2,7,128]{3,0,2,1:T(8,128)S(1)})) conditional(s32[]{:T(128)} %convert_element_type.48, (f32[192,2,7]{0,2,1:T(8,128)S(1)}, f32[192,2,7]{0,2,1:T(8,128)S(1)}, f32[192,2,7,128]{3,0,2,1:T(8,128)S(1)}) %tuple.53, (s32[1,512]{1,0:T(1,128)S(1)}, ...), branch_computations={%region_3.3_spmd, %region_4.6_spmd.clone} | conditional | flops 720575808 | bytes 21056228 | solution.py:44
  259.0 6.8 %conditional.3 = ((f32[192,2,7]{0,2,1:T(8,128)S(1)}, f32[192,2,7]{0,2,1:T(8,128)S(1)}, f32[192,2,7,128]{3,0,2,1:T(8,128)S(1)})) conditional(s32[]{:T(128)} %convert_element_type.48, (f32[192,2,7]{0,2,1:T(8,128)S(1)}, f32[192,2,7]{0,2,1:T(8,128)S(1)}, f32[192,2,7,128]{3,0,2,1:T(8,128)S(1)}) %tuple.53, (s32[1,512]{1,0:T(1,128)S(1)}, ...), branch_computations={%region_3.3_spmd, %region_4.6_spmd.clone} | conditional | flops 720575808 | bytes 21056228 | solution.py:44
  267.9 6.8 %conditional.3 = ((f32[192,2,7]{0,2,1:T(8,128)S(1)}, f32[192,2,7]{0,2,1:T(8,128)S(1)}, f32[192,2,7,128]{3,0,2,1:T(8,128)S(1)})) conditional(s32[]{:T(128)} %convert_element_type.48, (f32[192,2,7]{0,2,1:T(8,128)S(1)}, f32[192,2,7]{0,2,1:T(8,128)S(1)}, f32[192,2,7,128]{3,0,2,1:T(8,128)S(1)}) %tuple.53, (s32[1,512]{1,0:T(1,128)S(1)}, ...), branch_computations={%region_3.3_spmd, %region_4.6_spmd.clone} | conditional | flops 720575808 | bytes 21056228 | solution.py:44
  276.9 6.8 %conditional.3 = ((f32[192,2,7]{0,2,1:T(8,128)S(1)}, f32[192,2,7]{0,2,1:T(8,128)S(1)}, f32[192,2,7,128]{3,0,2,1:T(8,128)S(1)})) conditional(s32[]{:T(128)} %convert_element_type.48, (f32[192,2,7]{0,2,1:T(8,128)S(1)}, f32[192,2,7]{0,2,1:T(8,128)S(1)}, f32[192,2,7,128]{3,0,2,1:T(8,128)S(1)}) %tuple.53, (s32[1,512]{1,0:T(1,128)S(1)}, ...), branch_computations={%region_3.3_spmd, %region_4.6_spmd.clone} | conditional | flops 720575808 | bytes 21056228 | solution.py:44
  348.0 8.5 %fusion.42 = (f32[192]{0:T(256)S(1)}, bf16[192,3584]{1,0:T(8,128)(2,1)S(1)}) fusion(bf16[192,1792]{1,0:T(8,128)(2,1)S(1)} %convert_element_type.25, bf16[3584,3584]{1,0:T(8,128)(2,1)} %constant_dynamic-update-slice_fusion, s32[]{:T(128)S(6)} %select_n.88, bf16[192,3584]{1,0:T(8,128)(2,1)S(1)} %copy-done.19), kind=kOutput, calls=%fused_computation.44 | convolution fusion | flops 2470379264 | bytes 16286468 | tf_op jit(solution)/shard_map/dot_general | solution.py:118
  (196 shorter events, 183.8 us)
Async XLA Ops:
  7.2 214.9 %all-gather.3.cloned.1.call-start = ((), (), s32[]{:S(2)}) async-start(), calls=%async_computation | async-start | bytes 1671168 | tf_op jit(solution)/shard_map/all_gather | solution.py:96
  7.2 9.9 %collective-permute-start = (bf16[112,3584]{1,0:T(8,128)(2,1)}, bf16[112,3584]{1,0:T(8,128)(2,1)S(1)}, u32[]{:S(2)}, u32[]{:S(2)}) collective-permute-start(bf16[112,3584]{1,0:T(8,128)(2,1)} %param.16), channel_id=1, source_target_pairs={{0,1},{1,2},{2,3},{3,4},{4,5},{5,6},{6,7},{7,8},{8,9},{9,10},{10,1... | collective-permute-start | bytes 2408456 | tf_op jit(solution)/shard_map/ppermute | solution.py:114
  18.0 14.2 %collective-permute-start.1 = (bf16[112,3584]{1,0:T(8,128)(2,1)S(1)}, bf16[112,3584]{1,0:T(8,128)(2,1)S(1)}, u32[]{:S(2)}, u32[]{:S(2)}) collective-permute-start(bf16[112,3584]{1,0:T(8,128)(2,1)S(1)} %collective-permute-done), channel_id=1, source_target_pairs={{0,1},{1,2},{2,3},{3,4},{4,5},{5,6},{6,7},{7,8},{8,9},{9,10},{10,1... | collective-permute-start | bytes 2408456 | tf_op jit(solution)/shard_map/ppermute | solution.py:114
  33.1 14.3 %collective-permute-start.2 = (bf16[112,3584]{1,0:T(8,128)(2,1)S(1)}, bf16[112,3584]{1,0:T(8,128)(2,1)S(1)}, u32[]{:S(2)}, u32[]{:S(2)}) collective-permute-start(bf16[112,3584]{1,0:T(8,128)(2,1)S(1)} %collective-permute-done.1), channel_id=1, source_target_pairs={{0,1},{1,2},{2,3},{3,4},{4,5},{5,6},{6,7},{7,8},{8,9},{9,10},{10,1... | collective-permute-start | bytes 2408456 | tf_op jit(solution)/shard_map/ppermute | solution.py:114
  48.3 14.3 %collective-permute-start.3 = (bf16[112,3584]{1,0:T(8,128)(2,1)S(1)}, bf16[112,3584]{1,0:T(8,128)(2,1)S(1)}, u32[]{:S(2)}, u32[]{:S(2)}) collective-permute-start(bf16[112,3584]{1,0:T(8,128)(2,1)S(1)} %collective-permute-done.2), channel_id=1, source_target_pairs={{0,1},{1,2},{2,3},{3,4},{4,5},{5,6},{6,7},{7,8},{8,9},{9,10},{10,1... | collective-permute-start | bytes 2408456 | tf_op jit(solution)/shard_map/ppermute | solution.py:114
  63.5 14.3 %collective-permute-start.4 = (bf16[112,3584]{1,0:T(8,128)(2,1)S(1)}, bf16[112,3584]{1,0:T(8,128)(2,1)S(1)}, u32[]{:S(2)}, u32[]{:S(2)}) collective-permute-start(bf16[112,3584]{1,0:T(8,128)(2,1)S(1)} %collective-permute-done.3), channel_id=1, source_target_pairs={{0,1},{1,2},{2,3},{3,4},{4,5},{5,6},{6,7},{7,8},{8,9},{9,10},{10,1... | collective-permute-start | bytes 2408456 | tf_op jit(solution)/shard_map/ppermute | solution.py:114
  78.7 14.3 %collective-permute-start.5 = (bf16[112,3584]{1,0:T(8,128)(2,1)S(1)}, bf16[112,3584]{1,0:T(8,128)(2,1)S(1)}, u32[]{:S(2)}, u32[]{:S(2)}) collective-permute-start(bf16[112,3584]{1,0:T(8,128)(2,1)S(1)} %collective-permute-done.4), channel_id=1, source_target_pairs={{0,1},{1,2},{2,3},{3,4},{4,5},{5,6},{6,7},{7,8},{8,9},{9,10},{10,1... | collective-permute-start | bytes 2408456 | tf_op jit(solution)/shard_map/ppermute | solution.py:114
  93.0 123.0 %copy-start.8 = (bf16[112,3584]{1,0:T(8,128)(2,1)}, bf16[112,3584]{1,0:T(8,128)(2,1)S(1)}, u32[]{:S(2)}) copy-start(bf16[112,3584]{1,0:T(8,128)(2,1)S(1)} %collective-permute-done.5) | copy-start | bytes 2408452
  93.0 14.3 %collective-permute-start.6 = (bf16[112,3584]{1,0:T(8,128)(2,1)S(1)}, bf16[112,3584]{1,0:T(8,128)(2,1)S(1)}, u32[]{:S(2)}, u32[]{:S(2)}) collective-permute-start(bf16[112,3584]{1,0:T(8,128)(2,1)S(1)} %collective-permute-done.5), channel_id=1, source_target_pairs={{0,1},{1,2},{2,3},{3,4},{4,5},{5,6},{6,7},{7,8},{8,9},{9,10},{10,1... | collective-permute-start | bytes 2408456 | tf_op jit(solution)/shard_map/ppermute | solution.py:114
  98.2 127.7 %all-gather.5.cloned.1.call-start = ((), (), s32[]{:S(2)}) async-start(), calls=%async_computation.1 | async-start | bytes 1671168 | tf_op jit(solution)/shard_map/all_gather | solution.py:101
  107.3 114.7 %copy-start.9 = (bf16[112,3584]{1,0:T(8,128)(2,1)}, bf16[112,3584]{1,0:T(8,128)(2,1)S(1)}, u32[]{:S(2)}) copy-start(bf16[112,3584]{1,0:T(8,128)(2,1)S(1)} %collective-permute-done.6) | copy-start | bytes 2408452
  107.3 15.2 %collective-permute-start.7 = (bf16[112,3584]{1,0:T(8,128)(2,1)S(1)}, bf16[112,3584]{1,0:T(8,128)(2,1)S(1)}, u32[]{:S(2)}, u32[]{:S(2)}) collective-permute-start(bf16[112,3584]{1,0:T(8,128)(2,1)S(1)} %collective-permute-done.6), channel_id=1, source_target_pairs={{0,1},{1,2},{2,3},{3,4},{4,5},{5,6},{6,7},{7,8},{8,9},{9,10},{10,1... | collective-permute-start | bytes 2408456 | tf_op jit(solution)/shard_map/ppermute | solution.py:114
  123.4 20.6 %collective-permute-start.8 = (bf16[112,3584]{1,0:T(8,128)(2,1)S(1)}, bf16[112,3584]{1,0:T(8,128)(2,1)S(1)}, u32[]{:S(2)}, u32[]{:S(2)}) collective-permute-start(bf16[112,3584]{1,0:T(8,128)(2,1)S(1)} %collective-permute-done.7), channel_id=1, source_target_pairs={{0,1},{1,2},{2,3},{3,4},{4,5},{5,6},{6,7},{7,8},{8,9},{9,10},{10,1... | collective-permute-start | bytes 2408456 | tf_op jit(solution)/shard_map/ppermute | solution.py:114
  144.9 14.3 %collective-permute-start.9 = (bf16[112,3584]{1,0:T(8,128)(2,1)S(1)}, bf16[112,3584]{1,0:T(8,128)(2,1)S(1)}, u32[]{:S(2)}, u32[]{:S(2)}) collective-permute-start(bf16[112,3584]{1,0:T(8,128)(2,1)S(1)} %collective-permute-done.8), channel_id=1, source_target_pairs={{0,1},{1,2},{2,3},{3,4},{4,5},{5,6},{6,7},{7,8},{8,9},{9,10},{10,1... | collective-permute-start | bytes 2408456 | tf_op jit(solution)/shard_map/ppermute | solution.py:114
  159.2 62.9 %copy-start.12 = (bf16[112,3584]{1,0:T(8,128)(2,1)}, bf16[112,3584]{1,0:T(8,128)(2,1)S(1)}, u32[]{:S(2)}) copy-start(bf16[112,3584]{1,0:T(8,128)(2,1)S(1)} %collective-permute-done.9) | copy-start | bytes 2408452
  159.2 14.3 %collective-permute-start.10 = (bf16[112,3584]{1,0:T(8,128)(2,1)S(1)}, bf16[112,3584]{1,0:T(8,128)(2,1)S(1)}, u32[]{:S(2)}, u32[]{:S(2)}) collective-permute-start(bf16[112,3584]{1,0:T(8,128)(2,1)S(1)} %collective-permute-done.9), channel_id=1, source_target_pairs={{0,1},{1,2},{2,3},{3,4},{4,5},{5,6},{6,7},{7,8},{8,9},{9,10},{10,1... | collective-permute-start | bytes 2408456 | tf_op jit(solution)/shard_map/ppermute | solution.py:114
  173.5 56.6 %copy-start.13 = (bf16[112,3584]{1,0:T(8,128)(2,1)}, bf16[112,3584]{1,0:T(8,128)(2,1)S(1)}, u32[]{:S(2)}) copy-start(bf16[112,3584]{1,0:T(8,128)(2,1)S(1)} %collective-permute-done.10) | copy-start | bytes 2408452
  173.5 15.1 %collective-permute-start.11 = (bf16[112,3584]{1,0:T(8,128)(2,1)S(1)}, bf16[112,3584]{1,0:T(8,128)(2,1)S(1)}, u32[]{:S(2)}, u32[]{:S(2)}) collective-permute-start(bf16[112,3584]{1,0:T(8,128)(2,1)S(1)} %collective-permute-done.10), channel_id=1, source_target_pairs={{0,1},{1,2},{2,3},{3,4},{4,5},{5,6},{6,7},{7,8},{8,9},{9,10},{10,1... | collective-permute-start | bytes 2408456 | tf_op jit(solution)/shard_map/ppermute | solution.py:114
  189.5 20.6 %collective-permute-start.12 = (bf16[112,3584]{1,0:T(8,128)(2,1)S(1)}, bf16[112,3584]{1,0:T(8,128)(2,1)}, u32[]{:S(2)}, u32[]{:S(2)}) collective-permute-start(bf16[112,3584]{1,0:T(8,128)(2,1)S(1)} %collective-permute-done.11), channel_id=1, source_target_pairs={{0,1},{1,2},{2,3},{3,4},{4,5},{5,6},{6,7},{7,8},{8,9},{9,10},{10,1... | collective-permute-start | bytes 2408456 | tf_op jit(solution)/shard_map/ppermute | solution.py:114
  210.1 19.6 %collective-permute-start.13 = (bf16[112,3584]{1,0:T(8,128)(2,1)}, bf16[112,3584]{1,0:T(8,128)(2,1)}, u32[]{:S(2)}, u32[]{:S(2)}) collective-permute-start(bf16[112,3584]{1,0:T(8,128)(2,1)} %collective-permute-done.12), channel_id=1, source_target_pairs={{0,1},{1,2},{2,3},{3,4},{4,5},{5,6},{6,7},{7,8},{8,9},{9,10},{10,1... | collective-permute-start | bytes 2408456 | tf_op jit(solution)/shard_map/ppermute | solution.py:114
  229.7 57.8 %collective-permute-start.14 = (bf16[112,3584]{1,0:T(8,128)(2,1)}, bf16[112,3584]{1,0:T(8,128)(2,1)}, u32[]{:S(2)}, u32[]{:S(2)}) collective-permute-start(bf16[112,3584]{1,0:T(8,128)(2,1)} %collective-permute-done.13), channel_id=1, source_target_pairs={{0,1},{1,2},{2,3},{3,4},{4,5},{5,6},{6,7},{7,8},{8,9},{9,10},{10,1... | collective-permute-start | bytes 2408456 | tf_op jit(solution)/shard_map/ppermute | solution.py:114
  284.2 60.9 %copy-start.4 = (bf16[112,3584]{1,0:T(8,128)(2,1)S(1)}, bf16[112,3584]{1,0:T(8,128)(2,1)}, u32[]{:S(2)}) copy-start(bf16[112,3584]{1,0:T(8,128)(2,1)} %copy-done.3) | copy-start | bytes 2408452
  284.2 61.8 %copy-start.2 = (bf16[112,3584]{1,0:T(8,128)(2,1)S(1)}, bf16[112,3584]{1,0:T(8,128)(2,1)}, u32[]{:S(2)}) copy-start(bf16[112,3584]{1,0:T(8,128)(2,1)} %copy-done.1) | copy-start | bytes 2408452
  287.5 60.5 %copy-start.19 = (bf16[192,3584]{1,0:T(8,128)(2,1)S(1)}, bf16[192,3584]{1,0:T(8,128)(2,1)}, u32[]{:S(2)}) copy-start(bf16[192,3584]{1,0:T(8,128)(2,1)} %param.15) | copy-start | bytes 4128772
  (13 other events, 151.8 us)
Sparse Core Ops, SparseCore 0:
  98.3 46.9 all-gather.2
  164.5 46.7 all-gather.4
